TPU v7x, 32 devices: a whole 2x2x4 slice. The times are simulated.
32 devices in a mesh: fsdp: 8 (over z, y), tensor: 4 (over x, core).
Axes of the slice: x: 2, y: 2, z: 4, core: 2. Of those that a mesh axis runs over, the one named last changes fastest.
Arguments:
- tokens: bfloat16 [12288, 768], P(('fsdp', 'tensor')), may hold values from -6 to 6
- attn_weight: bfloat16 [3, 768, 768], P(None, 'fsdp', 'tensor'), may hold values from -0.21875 to 0.21875
- query_value_bias: bfloat16 [2, 12, 64], P(None, 'tensor', 'fsdp'), may hold values from -3 to 3
- out_weight: bfloat16 [768, 768], P('tensor', 'fsdp'), may hold values from -1.25 to 1.25
- hidden_weight: bfloat16 [768, 3072], P('fsdp', 'tensor'), may hold values from -0.21875 to 0.21875
- hidden_bias: bfloat16 [48, 64], P('tensor', 'fsdp'), may hold values from -3 to 3
- down_weight: bfloat16 [3072, 768], P('tensor', 'fsdp'), may hold values from -0.109375 to 0.109375
- norm_gains: bfloat16 [2, 768], P(None, 'fsdp'), may hold values from 0.5 to 1.5
- norm_biases: bfloat16 [2, 768], P(None, 'fsdp'), may hold values from -2 to 2
- output_biases: bfloat16 [2, 768], P(None, 'fsdp'), may hold values from -2 to 2
- segment_ids: int32 [12288], P('fsdp'), may hold values from 0 to 15, as said below
- padding: int32 [12288], P('fsdp'), may hold values from 0 to 1, as said below
- cotangent: bfloat16 [12288, 768], P(('fsdp', 'tensor')), may hold values from -6 to 6
Outputs:
- layer_out: bfloat16 [12288, 768], P(('fsdp', 'tensor'))
- tokens_grad: float32 [12288, 768], P(('fsdp', 'tensor'))
- attn_weight_grad: float32 [3, 768, 768], P(None, 'fsdp', 'tensor')
- query_value_bias_grad: float32 [2, 12, 64], P(None, 'tensor', 'fsdp')
- out_weight_grad: float32 [768, 768], P('tensor', 'fsdp')
- hidden_weight_grad: float32 [768, 3072], P('fsdp', 'tensor')
- hidden_bias_grad: float32 [48, 64], P('tensor', 'fsdp')
- down_weight_grad: float32 [3072, 768], P('tensor', 'fsdp')
- norm_gains_grad: float32 [2, 768], P(None, 'fsdp')
- norm_biases_grad: float32 [2, 768], P(None, 'fsdp')
- output_biases_grad: float32 [2, 768], P(None, 'fsdp')
- root_squares: float32 [3], replicated
Inputs may be any that keep to these rules, and one draw needn't show every extreme that they name: `segment_ids`: within each sequence of 1536 positions, segment ids start at 0 and rise by one at each new document; every document has 96 to 768 tokens except the last of a sequence, which its end may cut; some document has exactly 768 tokens. Within each sequence, the padding positions (value 0) form a tail of at most 192 positions.
All inputs are finite; a program needn't handle non-finite values.
Results may differ from a plain program's by a relative error of at most 0.013.
The roundings to bfloat16 on the way count: a program that leaves them out, or rounds other values in their place, can miss the bound.
Values may be sent and summed in bfloat16 or wider, within the bound.
A program may use at most 192 MiB of HBM per device.

v0:
```python
import jax
import jax.numpy as jnp
from jax import lax
from jax.sharding import PartitionSpec as P

D = 768
DH = 64


EPSILON = 1e-12


def split_up(value, dim, devices):
    before, after = (value.shape[:dim], value.shape[dim + 1 :])
    return jnp.moveaxis(value.reshape(*before, devices, -1, *after), dim, 0)


def summed_on_arrival(value, axis, dim):
    blocks = split_up(value, dim, lax.axis_size(axis))
    arrived = lax.all_to_all(blocks, axis, split_axis=0, concat_axis=0, tiled=True)
    return arrived.astype(jnp.float32).sum(axis=0)


def sent_together(arrays, axis, dim, along):
    ends, at = ([], 0)
    for a in arrays[:-1]:
        at += a.shape[along]
        ends.append(at)
    both = jnp.concatenate(arrays, axis=along)
    return tuple(jnp.split(summed_on_arrival(both, axis, dim), ends, axis=along))


def layer_norm(hidden, gain_row, shift_row):
    row_mean = jnp.mean(hidden, axis=-1, keepdims=True)
    centered = hidden - row_mean
    variance = jnp.mean(centered * centered, axis=-1, keepdims=True)
    return centered * lax.rsqrt(variance + EPSILON) * gain_row + shift_row


def gelu_exact(value):
    return jax.nn.gelu(value, approximate=False)


def shards(
    tokens,
    attn_weight,
    query_value_bias,
    out_weight,
    hidden_weight,
    hidden_bias,
    down_weight,
    norm_gains,
    norm_biases,
    output_biases,
    segment_ids,
    padding,
    cotangent,
):
    wide = jnp.float32
    narrow = jnp.bfloat16
    gathered = (
        lax.all_gather(attn_weight, "fsdp", axis=1, tiled=True),
        lax.all_gather(query_value_bias, "fsdp", axis=2, tiled=True),
        lax.all_gather(out_weight, "fsdp", axis=1, tiled=True),
        lax.all_gather(hidden_weight, "fsdp", axis=0, tiled=True),
        lax.all_gather(hidden_bias, "fsdp", axis=1, tiled=True),
        lax.all_gather(down_weight, "fsdp", axis=1, tiled=True),
        lax.all_gather(norm_gains, "fsdp", axis=1, tiled=True),
        lax.all_gather(norm_biases, "fsdp", axis=1, tiled=True),
        lax.all_gather(output_biases, "fsdp", axis=1, tiled=True),
    )
    w_qkv, qv_full, w_proj, w_up, up_bias, w_down, gain_rows, shift_rows, bias_rows = gathered
    row_count = tokens.shape[0]
    seq_len = segment_ids.shape[0]
    tensor_place = lax.axis_index("tensor")
    local_pad = lax.dynamic_slice_in_dim(padding, tensor_place * row_count, row_count, 0).astype(
        wide
    )
    whole_rows = lax.all_gather(tokens, "tensor", axis=0, tiled=True)
    width = w_qkv.shape[2]
    heads = width // DH
    projected = jnp.einsum("sd,jde->jse", whole_rows, w_qkv, preferred_element_type=wide)
    qv_flat = qv_full.astype(wide).reshape(2, width)
    queries = (projected[0] + qv_flat[0]).astype(narrow).reshape(seq_len, heads, DH)
    all_keys = projected[1].astype(narrow).reshape(seq_len, heads, DH)
    all_values = (projected[2] + qv_flat[1]).astype(narrow).reshape(seq_len, heads, DH)
    block_rows = min(512, seq_len)
    block_count = seq_len // block_rows
    positions = jnp.arange(seq_len, dtype=jnp.int32)
    key_live = padding == 1

    def scores_of(row_start):
        q_rows = lax.dynamic_slice_in_dim(queries, row_start, block_rows, 0)
        seg_rows = lax.dynamic_slice_in_dim(segment_ids, row_start, block_rows, 0)
        pos_rows = row_start + jnp.arange(block_rows, dtype=jnp.int32)
        allowed = (seg_rows[:, None] == segment_ids[None, :]) & key_live[None, :] | (
            pos_rows[:, None] == positions[None, :]
        )
        raw_scores = (
            jnp.einsum("qhd,khd->hqk", q_rows, all_keys, preferred_element_type=wide) * 0.125
        )
        return (q_rows, jnp.where(allowed[None], raw_scores, -1e30))

    def forward_block(block_index):
        row_start = block_index * block_rows
        q_rows, masked = scores_of(row_start)
        row_top = jnp.max(masked, axis=-1, keepdims=True)
        exp_terms = jnp.exp(masked - row_top)
        row_total = jnp.sum(exp_terms, axis=-1, keepdims=True)
        attn_probs = exp_terms / row_total
        pad_rows = lax.dynamic_slice_in_dim(padding, row_start, block_rows, 0).astype(wide)
        context = jnp.einsum(
            "hqk,khd->qhd", attn_probs.astype(narrow), all_values, preferred_element_type=wide
        )
        return (context * pad_rows[:, None, None], row_top[..., 0] + jnp.log(row_total[..., 0]))

    block_ids = jnp.arange(block_count, dtype=jnp.int32)
    contexts, log_totals = lax.map(forward_block, block_ids)
    context_low = contexts.reshape(seq_len, width).astype(narrow)
    attn_part = jnp.dot(context_low, w_proj, preferred_element_type=wide)
    attn_branch = lax.psum_scatter(
        attn_part, "tensor", scatter_dimension=0, tiled=True
    ) + bias_rows[0].astype(wide)
    input_rows = tokens.astype(wide)
    first_norm, first_pull = jax.vjp(
        layer_norm, input_rows + attn_branch, gain_rows[0].astype(wide), shift_rows[0].astype(wide)
    )
    up_use, down_use, up_bias_use = (w_up, w_down, up_bias)
    normed_all = lax.all_gather(first_norm.astype(narrow), "tensor", axis=0, tiled=True)
    pre_act = jnp.dot(normed_all, up_use, preferred_element_type=wide) + up_bias_use.astype(
        wide
    ).reshape(-1)
    acted, gelu_pull = jax.vjp(gelu_exact, pre_act)
    acted_low = acted.astype(narrow)
    ff_part = jnp.dot(acted_low, down_use, preferred_element_type=wide)
    ff_sum = lax.psum_scatter(
        ff_part.astype(jnp.bfloat16), "tensor", scatter_dimension=0, tiled=True
    ).astype(jnp.float32)
    ff_branch = ff_sum + bias_rows[1].astype(wide)
    layer_value, second_pull = jax.vjp(
        layer_norm, first_norm + ff_branch, gain_rows[1].astype(wide), shift_rows[1].astype(wide)
    )
    layer_out = layer_value.astype(narrow)
    live_col = local_pad[:, None]
    squares = jnp.stack(
        [
            jnp.sum(live_col * input_rows * input_rows),
            jnp.sum(live_col * attn_branch * attn_branch),
            jnp.sum(live_col * ff_branch * ff_branch),
        ]
    )
    square_sums, live_count = lax.psum((squares, jnp.sum(local_pad)), ("fsdp", "tensor"))
    root_values = jnp.sqrt(square_sums / (live_count * D))
    d_second, d_gain_two, d_shift_two = second_pull(cotangent.astype(wide))
    d_ff_low = d_second.astype(narrow)
    d_ff_bias = jnp.sum(d_ff_low.astype(wide), axis=0)
    d_ff_all = lax.all_gather(d_ff_low, "tensor", axis=0, tiled=True)
    d_down = jnp.einsum("sf,sd->fd", acted_low, d_ff_all, preferred_element_type=wide)
    d_acted = jnp.einsum("sd,fd->sf", d_ff_all, down_use, preferred_element_type=wide)
    d_pre_low = gelu_pull(d_acted)[0].astype(narrow)
    d_up_bias = jnp.sum(d_pre_low.astype(wide), axis=0).reshape(up_bias_use.shape)
    d_up = jnp.einsum("sd,sf->df", normed_all, d_pre_low, preferred_element_type=wide)
    d_norm_part = jnp.einsum("sf,df->sd", d_pre_low, up_use, preferred_element_type=wide)
    d_first_in = d_second + lax.psum_scatter(d_norm_part, "tensor", scatter_dimension=0, tiled=True)
    d_first, d_gain_one, d_shift_one = first_pull(d_first_in)
    d_attn_low = d_first.astype(narrow)
    d_attn_bias = jnp.sum(d_attn_low.astype(wide), axis=0)
    d_attn_all = lax.all_gather(d_attn_low, "tensor", axis=0, tiled=True)
    d_proj = jnp.einsum("se,sd->ed", context_low, d_attn_all, preferred_element_type=wide)
    d_context = jnp.einsum("sd,ed->se", d_attn_all, w_proj, preferred_element_type=wide).astype(
        narrow
    )
    d_context = d_context.reshape(seq_len, heads, DH)

    def backward_block(carried, block_index):
        d_keys_sum, d_values_sum = carried
        row_start = block_index * block_rows
        q_rows, masked = scores_of(row_start)
        attn_probs = jnp.exp(masked - log_totals[block_index][..., None])
        pad_rows = lax.dynamic_slice_in_dim(padding, row_start, block_rows, 0).astype(narrow)
        d_ctx_rows = (
            lax.dynamic_slice_in_dim(d_context, row_start, block_rows, 0) * pad_rows[:, None, None]
        )
        d_probs = jnp.einsum("qhd,khd->hqk", d_ctx_rows, all_values, preferred_element_type=wide)
        d_values_sum = d_values_sum + jnp.einsum(
            "hqk,qhd->khd", attn_probs.astype(narrow), d_ctx_rows, preferred_element_type=wide
        )
        inner_sum = jnp.sum(attn_probs * d_probs, axis=-1, keepdims=True)
        d_scores = (attn_probs * (d_probs - inner_sum)).astype(narrow)
        d_query_rows = (
            jnp.einsum("hqk,khd->qhd", d_scores, all_keys, preferred_element_type=wide) * 0.125
        )
        d_keys_sum = (
            d_keys_sum
            + jnp.einsum("hqk,qhd->khd", d_scores, q_rows, preferred_element_type=wide) * 0.125
        )
        return ((d_keys_sum, d_values_sum), d_query_rows)

    zero_heads = jnp.zeros((seq_len, heads, DH), wide)
    (d_keys_all, d_values_all), d_query_blocks = lax.scan(
        backward_block, (zero_heads, zero_heads), block_ids
    )
    d_qkv = jnp.stack(
        [
            d_query_blocks.reshape(seq_len, width),
            d_keys_all.reshape(seq_len, width),
            d_values_all.reshape(seq_len, width),
        ]
    ).astype(narrow)
    d_qkv_wide = d_qkv.astype(wide)
    d_qv_bias = jnp.stack([jnp.sum(d_qkv_wide[0], axis=0), jnp.sum(d_qkv_wide[2], axis=0)]).reshape(
        2, heads, DH
    )
    d_attn_weight = jnp.einsum("sd,jse->jde", whole_rows, d_qkv, preferred_element_type=wide)
    d_tokens_part = jnp.einsum("jse,jde->sd", d_qkv, w_qkv, preferred_element_type=wide)
    d_tokens = d_first + lax.psum_scatter(
        d_tokens_part.astype(jnp.bfloat16), "tensor", scatter_dimension=0, tiled=True
    ).astype(jnp.float32)
    gain_terms, shift_terms, bias_terms = lax.psum(
        (
            jnp.stack([d_gain_one, d_gain_two]),
            jnp.stack([d_shift_one, d_shift_two]),
            jnp.stack([d_attn_bias, d_ff_bias]),
        ),
        "tensor",
    )
    grads = (
        summed_on_arrival(d_attn_weight.astype(jnp.bfloat16), "fsdp", 1),
        summed_on_arrival(d_qv_bias.astype(jnp.bfloat16), "fsdp", 2),
        summed_on_arrival(d_proj.astype(jnp.bfloat16), "fsdp", 1),
        summed_on_arrival(d_up.astype(jnp.bfloat16), "fsdp", 0),
        summed_on_arrival(d_up_bias.astype(jnp.bfloat16), "fsdp", 1),
        *sent_together(
            (
                d_down.astype(jnp.bfloat16),
                gain_terms.astype(jnp.bfloat16),
                shift_terms.astype(jnp.bfloat16),
                bias_terms.astype(jnp.bfloat16),
            ),
            "fsdp",
            1,
            0,
        ),
    )
    return (
        layer_out,
        d_tokens,
        grads[0],
        grads[1],
        grads[2],
        grads[3],
        grads[4],
        grads[5],
        grads[6],
        grads[7],
        grads[8],
        root_values,
    )


def solution(mesh):
    placed = (
        P(("fsdp", "tensor"), None),
        P(None, "fsdp", "tensor"),
        P(None, "tensor", "fsdp"),
        P("tensor", "fsdp"),
        P("fsdp", "tensor"),
        P("tensor", "fsdp"),
        P("tensor", "fsdp"),
        P(None, "fsdp"),
        P(None, "fsdp"),
        P(None, "fsdp"),
        P("fsdp"),
        P("fsdp"),
        P(("fsdp", "tensor"), None),
    )
    return jax.shard_map(
        shards,
        mesh=mesh,
        in_specs=placed,
        out_specs=(
            P(("fsdp", "tensor"), None),
            P(("fsdp", "tensor"), None),
            P(None, "fsdp", "tensor"),
            P(None, "tensor", "fsdp"),
            P("tensor", "fsdp"),
            P("fsdp", "tensor"),
            P("tensor", "fsdp"),
            P("tensor", "fsdp"),
            P(None, "fsdp"),
            P(None, "fsdp"),
            P(None, "fsdp"),
            P(),
        ),
        check_vma=False,
    )
```

profile of v0, /device:TPU:0, one launch (start us, length us, event | category | flops | bytes accessed | tf_op | source)
XLA Modules:
  0.0 712.1 jit_solution(12690553113881603985)
XLA Ops:
  9.6 32.4 %all_gather.41 = bf16[2,3,64]{1,0,2:T(2,128)(2,1)S(1)} all-gather(bf16[2,3,8]{1,0,2:T(2,128)(2,1)S(1)} %copy.145), channel_id=1, replica_groups=mesh['fsdp'=8,'tensor'=4] {'fsdp'}, dimensions={2}, use_global_device_ids=true | all-gather | bytes 864 | tf_op jit(solution)/shard_map/all_gather | solution.py:63
  44.1 31.5 %all_gather.42 = bf16[192,768]{0,1:T(8,128)(2,1)S(1)} all-gather(bf16[192,96]{0,1:T(8,128)(2,1)S(1)} %copy.149), channel_id=1, replica_groups=mesh['fsdp'=8,'tensor'=4] {'fsdp'}, dimensions={1}, use_global_device_ids=true | all-gather | bytes 331776 | tf_op jit(solution)/shard_map/all_gather | solution.py:64
  76.4 38.2 %all_gather.39 = bf16[3,768,192]{2,0,1:T(4,128)(2,1)} all-gather(bf16[3,96,192]{2,0,1:T(4,128)(2,1)S(1)} %copy.143), channel_id=1, replica_groups=mesh['fsdp'=8,'tensor'=4] {'fsdp'}, dimensions={1}, use_global_device_ids=true | all-gather | bytes 995328 | tf_op jit(solution)/shard_map/all_gather | solution.py:62
  114.6 4.3 convolution_bitcast_fusion
  119.8 34.3 %while.28 = (s32[]{:T(128)}, bf16[3,512,3,64]{1,3,2,0:T(8,128)(2,1)S(1)}, f32[3,3,512]{2,1,0:T(4,128)}, s32[3]{0:T(128)S(1)}, s32[1536]{0:T(1024)S(1)}, /*index=...) while((s32[]{:T(128)}, ...), condition=%wide.region_3.4_spmd.clone, body=%wide.region_0.3_spmd.clone.sunk | while | flops 635534848 | bytes 33306336 | solution.py:118
  127.0 3.6 fusion.134
  138.4 3.6 fusion.134
  149.8 3.6 fusion.134
  155.6 3.0 fusion.84
  159.2 17.5 %all-gather.1 = bf16[8,96,2]{1,2,0:T(2,128)(2,1)S(1)} all-gather(bf16[1,96,2]{1,2,0:T(2,128)(2,1)S(1)} %bitcast.168), channel_id=1, replica_groups=mesh['fsdp'=8,'tensor'=4] {'fsdp'}, dimensions={0}, use_global_device_ids=true | all-gather | bytes 3456 | tf_op jit(solution)/shard_map/all_gather | solution.py:68
  176.9 17.1 %all-gather.2 = bf16[8,96,2]{1,2,0:T(2,128)(2,1)S(1)} all-gather(bf16[1,96,2]{1,2,0:T(2,128)(2,1)S(1)} %bitcast.169), channel_id=1, replica_groups=mesh['fsdp'=8,'tensor'=4] {'fsdp'}, dimensions={0}, use_global_device_ids=true | all-gather | bytes 3456 | tf_op jit(solution)/shard_map/all_gather | solution.py:69
  194.1 17.7 %all-gather = bf16[8,96,2]{1,2,0:T(2,128)(2,1)S(1)} all-gather(bf16[1,96,2]{1,2,0:T(2,128)(2,1)S(1)} %bitcast.170), channel_id=1, replica_groups=mesh['fsdp'=8,'tensor'=4] {'fsdp'}, dimensions={0}, use_global_device_ids=true | all-gather | bytes 3456 | tf_op jit(solution)/shard_map/all_gather | solution.py:70
  216.2 26.6 %all_gather.48 = bf16[12,64]{0,1:T(8,128)(2,1)S(1)} all-gather(bf16[12,8]{0,1:T(8,128)(2,1)S(1)} %copy-done.37), channel_id=1, replica_groups=mesh['fsdp'=8,'tensor'=4] {'fsdp'}, dimensions={1}, use_global_device_ids=true | all-gather | bytes 1728 | tf_op jit(solution)/shard_map/all_gather | solution.py:66
  242.9 15.1 %multiply_convert_fusion.1 = (bf16[1536,768]{1,0:T(8,128)(2,1)}, f32[1536,768]{1,0:T(8,128)}, f32[1536,768]{1,0:T(8,128)}) fusion(f32[768]{0:T(1024)S(1)} %reshape.337, bf16[1536,768]{1,0:T(8,128)(2,1)} %all-gather.12.cloned.1.call-done, bf16[768,768]{1,0:T(8,128)(2,1)} %all-gather.14.cloned.1.call-done), kind=kOutput, calls=%fused_computation.53 | convolution fusion | flops 1889796096 | bytes 15338496 | tf_op jit(solution)/shard_map/dot_general | solution.py:130
  258.0 22.3 %all-gather.16.cloned.1.call-done = bf16[768,768]{0,1:T(8,128)(2,1)} async-done(((bf16[768,96]{0,1:T(8,128)(2,1)}), bf16[768,768]{0,1:T(8,128)(2,1)}) %all-gather.16.cloned.1.call-update) | async-done | bytes 1179664 | tf_op jit(solution)/shard_map/all_gather | solution.py:67
  280.3 5.4 convolution_convert_fusion
  286.5 30.4 %reduce-scatter.7.cloned.1.call-done = bf16[384,768]{1,0:T(8,128)(2,1)} async-done(((bf16[1536,768]{1,0:T(8,128)(2,1)}), bf16[384,768]{1,0:T(8,128)(2,1)}) %reduce-scatter.7.cloned.1.call-update) | async-done | bytes 589840 | tf_op jit(solution)/shard_map/reduce_scatter | solution.py:136
  316.9 3.2 fusion.57
  326.0 23.8 %all-gather.18.cloned.1.call-done = bf16[1536,768]{1,0:T(8,128)(2,1)} async-done(((bf16[384,768]{1,0:T(8,128)(2,1)}), bf16[1536,768]{1,0:T(8,128)(2,1)}) %all-gather.18.cloned.1.call-update) | async-done | bytes 2359312 | tf_op jit(solution)/shard_map/all_gather | solution.py:157
  349.8 8.8 %fusion.74 = (bf16[768]{0:T(1024)(128)(2,1)}, bf16[1536,768]{1,0:T(8,128)(2,1)S(1)}) fusion(f32[1536,768]{1,0:T(8,128)} %get-tuple-element.383, f32[1536,768]{1,0:T(8,128)} %get-tuple-element.400, f32[768]{0:T(1024)} %copy-done.35, bf16[1536,768]{1,0:T(8,128)(2,1)} %all-gather.18.cloned.1.call-done, bf16[768,768]{0,1:T(8,128)(2,1)} %all-gather.16.cloned.1.call-done), kind=kOutput, calls=%fused_computation.158 | convolution fusion | flops 1830812928 | bytes 15340032 | tf_op jit(solution)/shard_map/sd,fd->sf/dot_general | solution.py:159
  360.0 4.2 fusion.85
  364.3 48.1 %reduce-scatter.9.cloned.1.call-done = f32[384,768]{1,0:T(8,128)} async-done(((f32[1536,768]{1,0:T(8,128)}), f32[384,768]{1,0:T(8,128)}) %reduce-scatter.9.cloned.1.call-update) | async-done | bytes 1179664 | tf_op jit(solution)/shard_map/reduce_scatter | solution.py:164
  424.7 5.5 all-to-all-start.4
  430.3 5.6 convolution_convert_fusion.2
  435.9 3.1 convolution_convert_fusion.3
  440.9 11.6 %all-reduce.1 = (bf16[2,768]{1,0:T(2,128)(2,1)}, bf16[2,768]{1,0:T(2,128)(2,1)}, bf16[2,768]{1,0:T(2,128)(2,1)}) all-reduce(f32[2,768]{1,0:T(2,128)} %pad_maximum_fusion.4, f32[2,768]{1,0:T(2,128)} %pad_maximum_fusion.3, f32[2,768]{1,0:T(2,128)} %pad_maximum_fusion.2), channel_id=1, replica_groups=mesh['fsdp'=8,'tensor'=4] {'tensor'}, use_global_device_ids=true, to_apply=%region_35.36 | all-reduce | flops 4608 | bytes 27648 | tf_op jit(solution)/shard_map/psum | solution.py:219
  452.5 3.5 convolution_convert_fusion.1
  456.0 6.0 all-to-all-start.3
  463.1 101.5 %while.29 = (s32[]{:T(128)}, f32[1536,3,64]{0,2,1:T(8,128)S(1)}, f32[1536,3,64]{0,2,1:T(8,128)S(1)}, bf16[3,512,3,64]{1,3,2,0:T(8,128)(2,1)}, s32[3]{0:T(128)S(1...) while((s32[]{:T(128)}, f32[1536,3,64]{0,2,1:T(8,128)S(1)}, ...), condition=%wide.region_17.18_spmd.clone, body=%wide.region_15.17_spmd.clone.sunk | while | flops 1536687616 | bytes 141431936 | solution.py:200
  471.2 7.2 %multiply_reduce_fusion.6 = (f32[3,512]{1,0:T(4,128)S(1)}, f32[3,512,1536]{2,1,0:T(8,128)}) fusion(f32[3,512,1536]{2,1,0:T(8,128)S(1)} %fusion.142, f32[3,512]{1,0:T(4,128)S(1)} %dynamic-slice_bitcast_fusion.2, bf16[1536,3,64]{0,2,1:T(8,128)(2,1)S(1)} %get-tuple-element.637, bf16[1536,3,64]{0,2,1:T(8,128)(2,1)} %get-tuple-element.634, ...), kind=kOutput, calls=%fused_computation.22.clone.1 | convolution fusion | flops 313784832 | bytes 20459524 | tf_op jit(solution)/shard_map/while/body/eval_jaxpr/qhd,khd->hqk/dot_general | solution.py:100
  478.5 9.4 %multiply_convert_fusion.3 = bf16[3,512,1536]{2,1,0:T(8,128)(2,1)} fusion(f32[3,512,1536]{2,1,0:T(8,128)} %get-tuple-element.549, f32[3,512,1536]{2,1,0:T(8,128)} %copy-done, f32[3,512]{1,0:T(4,128)S(1)} %get-tuple-element.550), kind=kLoop, calls=%fused_computation.21.clone.1 | loop fusion | flops 7077888 | bytes 23599104 | tf_op jit(solution)/shard_map/while/body/eval_jaxpr/convert_element_type | solution.py:189
  487.9 5.0 fusion.145
  505.1 7.2 %multiply_reduce_fusion.6 = (f32[3,512]{1,0:T(4,128)S(1)}, f32[3,512,1536]{2,1,0:T(8,128)}) fusion(f32[3,512,1536]{2,1,0:T(8,128)S(1)} %fusion.142, f32[3,512]{1,0:T(4,128)S(1)} %dynamic-slice_bitcast_fusion.2, bf16[1536,3,64]{0,2,1:T(8,128)(2,1)S(1)} %get-tuple-element.637, bf16[1536,3,64]{0,2,1:T(8,128)(2,1)} %get-tuple-element.634, ...), kind=kOutput, calls=%fused_computation.22.clone.1 | convolution fusion | flops 313784832 | bytes 20459524 | tf_op jit(solution)/shard_map/while/body/eval_jaxpr/qhd,khd->hqk/dot_general | solution.py:100
  512.3 9.4 %multiply_convert_fusion.3 = bf16[3,512,1536]{2,1,0:T(8,128)(2,1)} fusion(f32[3,512,1536]{2,1,0:T(8,128)} %get-tuple-element.549, f32[3,512,1536]{2,1,0:T(8,128)} %copy-done, f32[3,512]{1,0:T(4,128)S(1)} %get-tuple-element.550), kind=kLoop, calls=%fused_computation.21.clone.1 | loop fusion | flops 7077888 | bytes 23599104 | tf_op jit(solution)/shard_map/while/body/eval_jaxpr/convert_element_type | solution.py:189
  521.7 5.0 fusion.145
  538.9 7.2 %multiply_reduce_fusion.6 = (f32[3,512]{1,0:T(4,128)S(1)}, f32[3,512,1536]{2,1,0:T(8,128)}) fusion(f32[3,512,1536]{2,1,0:T(8,128)S(1)} %fusion.142, f32[3,512]{1,0:T(4,128)S(1)} %dynamic-slice_bitcast_fusion.2, bf16[1536,3,64]{0,2,1:T(8,128)(2,1)S(1)} %get-tuple-element.637, bf16[1536,3,64]{0,2,1:T(8,128)(2,1)} %get-tuple-element.634, ...), kind=kOutput, calls=%fused_computation.22.clone.1 | convolution fusion | flops 313784832 | bytes 20459524 | tf_op jit(solution)/shard_map/while/body/eval_jaxpr/qhd,khd->hqk/dot_general | solution.py:100
  546.1 9.4 %multiply_convert_fusion.3 = bf16[3,512,1536]{2,1,0:T(8,128)(2,1)} fusion(f32[3,512,1536]{2,1,0:T(8,128)} %get-tuple-element.549, f32[3,512,1536]{2,1,0:T(8,128)} %copy-done, f32[3,512]{1,0:T(4,128)S(1)} %get-tuple-element.550), kind=kLoop, calls=%fused_computation.21.clone.1 | loop fusion | flops 7077888 | bytes 23599104 | tf_op jit(solution)/shard_map/while/body/eval_jaxpr/convert_element_type | solution.py:189
  555.6 5.0 fusion.145
  569.3 3.5 bitcast_convert_fusion
  576.4 6.0 all-to-all-start.5
  583.7 30.8 %all-to-all-done.5 = bf16[8,774,96]{1,2,0:T(8,128)(2,1)S(1)} async-done(((bf16[8,774,96]{1,2,0:T(8,128)(2,1)}), bf16[8,774,96]{1,2,0:T(8,128)(2,1)S(1)}, u32[]{:S(2)}, u32[]{:S(2)}) %all-to-all-start.5) | async-done | bytes 1188896 | tf_op jit(solution)/shard_map/all_to_all | solution.py:20
  614.5 3.7 all-to-all-start.1
  621.8 2.9 all-to-all-done.1
  624.7 3.5 all-to-all-start.2
  628.2 4.3 fusion.52
  636.2 2.9 all-to-all-done.2
  639.1 4.2 all-to-all-start
  645.4 45.6 %all-reduce = (f32[3]{0:T(128)S(1)}, f32[]{:T(128)}) all-reduce(f32[3]{0:T(128)S(1)} %pad_maximum_fusion.5, f32[]{:T(128)} %get-tuple-element.367), channel_id=1, replica_groups=mesh['fsdp'=8,'tensor'=4] {'fsdp','tensor'}, use_global_device_ids=true, to_apply=%region_40.41 | all-reduce | flops 4 | bytes 32 | tf_op jit(solution)/shard_map/psum | solution.py:152
  (303 shorter events, 116.8 us)
Async XLA Ops:
  8.0 106.5 %all-gather.10.cloned.1.call-start = ((), (), s32[]{:S(2)}) async-start(), calls=%async_computation.10 | async-start | bytes 2949120 | tf_op jit(solution)/shard_map/all_gather | solution.py:79
  8.7 203.8 %reduce-scatter.5.cloned.1.call-start = ((), (), s32[]{:S(2)}) async-start(), calls=%async_computation.11 | async-start | bytes 5898240 | tf_op jit(solution)/shard_map/reduce_scatter | solution.py:121
  75.7 79.1 %copy-start.6 = (bf16[192,768]{0,1:T(8,128)(2,1)}, bf16[192,768]{0,1:T(8,128)(2,1)S(1)}, u32[]{:S(2)}) copy-start(bf16[192,768]{0,1:T(8,128)(2,1)S(1)} %all_gather.42) | copy-start | bytes 884740
  154.1 4.5 copy-start.2
  158.6 18.3 %copy-start.39 = (bf16[2,96]{1,0:T(2,128)(2,1)S(1)}, bf16[2,96]{1,0:T(2,128)(2,1)}, u32[]{:S(2)}) copy-start(bf16[2,96]{1,0:T(2,128)(2,1)} %param.25) | copy-start | bytes 1156
  158.6 35.5 %copy-start.40 = (bf16[2,96]{1,0:T(2,128)(2,1)S(1)}, bf16[2,96]{1,0:T(2,128)(2,1)}, u32[]{:S(2)}) copy-start(bf16[2,96]{1,0:T(2,128)(2,1)} %param.26) | copy-start | bytes 1156
  158.6 54.0 %copy-start.5 = (bf16[384,768]{1,0:T(8,128)(2,1)S(1)}, bf16[384,768]{1,0:T(8,128)(2,1)}, u32[]{:S(2)}) copy-start(bf16[384,768]{1,0:T(8,128)(2,1)} %param.17) | copy-start | bytes 1769476
  158.6 84.3 %all-gather.14.cloned.1.call-start = ((), (), s32[]{:S(2)}) async-start(), calls=%async_computation.13 | async-start | bytes 1327104 | tf_op jit(solution)/shard_map/all_gather | solution.py:65
  159.2 83.7 %all-gather.12.cloned.1.call-start = ((), (), s32[]{:S(2)}) async-start(), calls=%async_computation.12 | async-start | bytes 2949120 | tf_op jit(solution)/shard_map/all_gather | solution.py:129
  212.5 107.9 %copy-start.23 = (f32[768]{0:T(1024)}, f32[768]{0:T(1024)S(1)}, u32[]{:S(2)}) copy-start(f32[768]{0:T(1024)S(1)} %get-tuple-element.307) | copy-start | bytes 9220
  214.1 102.8 %copy-start.21 = (f32[384]{0:T(512)}, f32[384]{0:T(512)S(1)}, u32[]{:S(2)}) copy-start(f32[384]{0:T(512)S(1)} %broadcast_multiply_fusion.1) | copy-start | bytes 4612
  214.4 102.5 %copy-start.22 = (f32[384]{0:T(512)}, f32[384]{0:T(512)S(1)}, u32[]{:S(2)}) copy-start(f32[384]{0:T(512)S(1)} %fusion.70) | copy-start | bytes 4612
  215.5 64.8 %all-gather.16.cloned.1.call-start = ((), (), s32[]{:S(2)}) async-start(), calls=%async_computation.14 | async-start | bytes 1327104 | tf_op jit(solution)/shard_map/all_gather | solution.py:67
  216.1 100.8 %reduce-scatter.7.cloned.1.call-start = ((), (), s32[]{:S(2)}) async-start(), calls=%async_computation.15 | async-start | bytes 2949120 | tf_op jit(solution)/shard_map/reduce_scatter | solution.py:136
  242.9 15.1 %copy-start.35 = (f32[768]{0:T(1024)}, f32[768]{0:T(1024)S(1)}, u32[]{:S(2)}) copy-start(f32[768]{0:T(1024)S(1)} %reshape.337) | copy-start | bytes 9220
  285.7 64.1 %all-gather.18.cloned.1.call-start = ((), (), s32[]{:S(2)}) async-start(), calls=%async_computation.16 | async-start | bytes 2949120 | tf_op jit(solution)/shard_map/all_gather | solution.py:157
  325.8 86.6 %reduce-scatter.9.cloned.1.call-start = ((), (), s32[]{:S(2)}) async-start(), calls=%async_computation.17 | async-start | bytes 5898240 | tf_op jit(solution)/shard_map/reduce_scatter | solution.py:164
  349.8 10.2 %copy-start.42 = (bf16[768,768]{1,0:T(8,128)(2,1)S(1)}, bf16[768,768]{1,0:T(8,128)(2,1)}, u32[]{:S(2)}) copy-start(bf16[768,768]{1,0:T(8,128)(2,1)} %all-gather.14.cloned.1.call-done) | copy-start | bytes 3538948
  364.2 88.3 %all-gather.20.cloned.1.call-start = ((), (), s32[]{:S(2)}) async-start(), calls=%async_computation.18 | async-start | bytes 2949120 | tf_op jit(solution)/shard_map/all_gather | solution.py:168
  416.7 4.0 copy-start.29
  424.7 31.3 %all-to-all-start.4 = ((bf16[8,12,8]{1,2,0:T(8,128)(2,1)}), bf16[8,12,8]{1,2,0:T(8,128)(2,1)}, u32[]{:S(2)}, u32[]{:S(2)}) async-start(bf16[8,12,8]{1,2,0:T(8,128)(2,1)} %copy.162), calls=%async_computation.8 | async-start | bytes 32768 | tf_op jit(solution)/shard_map/all_to_all | solution.py:20
  430.2 5.6 copy-start.41
  430.2 5.6 copy-start.46
  456.0 120.5 %all-to-all-start.3 = ((bf16[8,96,768]{2,1,0:T(8,128)(2,1)}), bf16[8,96,768]{2,1,0:T(8,128)(2,1)}, u32[]{:S(2)}, u32[]{:S(2)}) async-start(bf16[8,96,768]{2,1,0:T(8,128)(2,1)} %bitcast.161), calls=%async_computation.7 | async-start | bytes 2359296 | tf_op jit(solution)/shard_map/all_to_all | solution.py:20
  462.0 240.3 %reduce-scatter.11.cloned.1.call-start = ((), (), s32[]{:S(2)}) async-start(), calls=%async_computation.19 | async-start | bytes 2949120 | tf_op jit(solution)/shard_map/reduce_scatter | solution.py:216
  463.1 5.7 copy-start.18
  463.1 5.7 copy-start.43
  471.2 7.2 %copy-start = (f32[3,512,1536]{2,1,0:T(8,128)}, f32[3,512,1536]{2,1,0:T(8,128)S(1)}, u32[]{:S(2)}) copy-start(f32[3,512,1536]{2,1,0:T(8,128)S(1)} %fusion.142) | copy-start | bytes 28311556 | tf_op jit(solution)/shard_map/while
  487.9 5.1 copy-start.1
  487.9 5.3 copy-start.8
  496.9 5.7 copy-start.18
  496.9 5.7 copy-start.43
  505.1 7.2 %copy-start = (f32[3,512,1536]{2,1,0:T(8,128)}, f32[3,512,1536]{2,1,0:T(8,128)S(1)}, u32[]{:S(2)}) copy-start(f32[3,512,1536]{2,1,0:T(8,128)S(1)} %fusion.142) | copy-start | bytes 28311556 | tf_op jit(solution)/shard_map/while
  521.7 5.1 copy-start.1
  521.7 5.3 copy-start.8
  530.8 5.7 copy-start.18
  530.8 5.7 copy-start.43
  538.9 7.2 %copy-start = (f32[3,512,1536]{2,1,0:T(8,128)}, f32[3,512,1536]{2,1,0:T(8,128)S(1)}, u32[]{:S(2)}) copy-start(f32[3,512,1536]{2,1,0:T(8,128)S(1)} %fusion.142) | copy-start | bytes 28311556 | tf_op jit(solution)/shard_map/while
  555.6 5.1 copy-start.1
  555.6 5.3 copy-start.8
  574.9 7.5 %copy-start.13 = (bf16[1,1536,192]{1,2,0:T(8,128)(2,1)S(1)}, bf16[1,1536,192]{1,2,0:T(8,128)(2,1)}, u32[]{:S(2)}) copy-start(bf16[1,1536,192]{1,2,0:T(8,128)(2,1)} %stack_reshape.12) | copy-start | bytes 1769476
  576.4 38.1 %all-to-all-start.5 = ((bf16[8,774,96]{1,2,0:T(8,128)(2,1)}), bf16[8,774,96]{1,2,0:T(8,128)(2,1)S(1)}, u32[]{:S(2)}, u32[]{:S(2)}) async-start(bf16[8,774,96]{1,2,0:T(8,128)(2,1)} %bitcast.149), calls=%async_computation.9 | async-start | bytes 2752512 | tf_op jit(solution)/shard_map/all_to_all | solution.py:20
  582.7 35.5 %copy-start.11 = (bf16[24,8,3,512]{3,1,2,0:T(8,128)(2,1)S(1)}, bf16[24,8,3,512]{3,1,2,0:T(8,128)(2,1)}, u32[]{:S(2)}) copy-start(bf16[24,8,3,512]{3,1,2,0:T(8,128)(2,1)} %copy-done.10) | copy-start | bytes 1769476
  614.5 10.2 %all-to-all-start.1 = ((bf16[8,2,3,8]{3,1,2,0:T(2,128)(2,1)}), bf16[8,2,3,8]{3,1,2,0:T(2,128)(2,1)S(1)}, u32[]{:S(2)}, u32[]{:S(2)}) async-start(bf16[8,2,3,8]{3,1,2,0:T(2,128)(2,1)} %copy.158), calls=%async_computation.5 | async-start | bytes 24576 | tf_op jit(solution)/shard_map/all_to_all | solution.py:20
  624.7 14.4 %all-to-all-start.2 = ((bf16[8,192,96]{2,1,0:T(8,128)(2,1)}), bf16[8,192,96]{2,1,0:T(8,128)(2,1)S(1)}, u32[]{:S(2)}, u32[]{:S(2)}) async-start(bf16[8,192,96]{2,1,0:T(8,128)(2,1)} %bitcast.116), calls=%async_computation.6 | async-start | bytes 786432 | tf_op jit(solution)/shard_map/all_to_all | solution.py:20
  639.1 60.7 %all-to-all-start = ((bf16[8,3,96,192]{2,3,1,0:T(8,128)(2,1)}), bf16[8,3,96,192]{2,3,1,0:T(8,128)(2,1)}, u32[]{:S(2)}, u32[]{:S(2)}) async-start(bf16[8,3,96,192]{2,3,1,0:T(8,128)(2,1)} %bitcast.115), calls=%async_computation.4 | async-start | bytes 2359296 | tf_op jit(solution)/shard_map/all_to_all | solution.py:20
  695.6 6.7 copy-start.4
  695.6 6.7 copy-start.26
  (33 other events, 63.8 us)
Sparse Core Ops, SparseCore 0:
  10.4 26.7 all-gather.9
  158.7 45.7 reduce-scatter.4
  364.3 47.9 reduce-scatter.8
Sparse Core Ops, SparseCore 1:
  161.3 39.2 all-gather.13
  215.6 21.1 all-gather.11
  238.8 41.4 all-gather.15
  285.8 31.0 reduce-scatter.6
  325.9 23.9 all-gather.17
  419.4 23.9 all-gather.19
  572.9 33.1 reduce-scatter.10
where the time goes:
time: 722 us; the launch traced here: 712 us
  blocking collectives  238 us (33%)
  waiting for transfers between devices  163 us (23%)
  matrix products  135 us (19%)
  other arithmetic  80.1 us (11%)
  local copies, waits for them, and re-layouts  39.1 us (5%)
  starting transfers between devices  29.7 us (4%)
  between operations  17 us (2%)
  loops' own time  10.2 us (1%)
    reduce_scatter x1, waiting for transfers between devices, shards(): lax.psum_scatter(d_norm_part, 'tensor', scatter_dimension=0, tiled=True)  48.1 us
    psum x1, blocking collectives, shards(): lax.psum((squares, jnp.sum(local_pad)), ('fsdp', 'tensor'))  45.6 us
    all_gather x1, blocking collectives, shards(): lax.all_gather(attn_weight, 'fsdp', axis=1, tiled=True)  38.2 us
    all_to_all x6, waiting for transfers between devices, summed_on_arrival(): lax.all_to_all(blocks, axis, split_axis=0, concat_axis=0, tiled=True)  36.7 us
    all_gather x1, blocking collectives, shards(): lax.all_gather(query_value_bias, 'fsdp', axis=2, tiled=True)  32.4 us
    all_gather x1, blocking collectives, shards(): lax.all_gather(out_weight, 'fsdp', axis=1, tiled=True)  31.5 us
    reduce_scatter x1, waiting for transfers between devices, shards(): lax.psum_scatter(ff_part.astype(jnp.bfloat16), 'tensor', scatter_dimensio...  30.4 us
    all_to_all x6, starting transfers between devices, summed_on_arrival(): lax.all_to_all(blocks, axis, split_axis=0, concat_axis=0, tiled=True)  28.9 us
  transfers between devices with their start and end apart: 16, of which 7 were waited for; matrix products, arithmetic and copies ran while one was open for 24% of the time, Pallas kernels for 0%

commit v1 on v0

v1 whole, which is shorter than its diff:
```python
import functools

import jax
import jax.numpy as jnp
from jax import lax
from jax.experimental import pallas as pl
from jax.experimental.pallas import tpu as pltpu
from jax.sharding import PartitionSpec as P

MESH = pl.DeviceIdType.MESH
DH = 64
EPSILON = 1e-12
MASKED = -1e30
DOC_MOST = 768
BLK = 256
LN_ROWS = 64
wide = jnp.float32
narrow = jnp.bfloat16

PARTS = ("qkv", "out", "up", "down")


def nn(a, b):
    return lax.dot_general(a, b, (((1,), (0,)), ((), ())), preferred_element_type=wide)


def nt(a, b):
    return lax.dot_general(a, b, (((1,), (1,)), ((), ())), preferred_element_type=wide)


def tn(a, b):
    return lax.dot_general(a, b, (((0,), (0,)), ((), ())), preferred_element_type=wide)


def layer_kernel(sizes, *refs):
    fused, n_f, D, F, S, heads, pad_w, shard = sizes
    R = S // 4
    names = list(NAMES_IN) + list(NAMES_OUT) + list(NAMES_SCRATCH)
    r = dict(zip(names, refs))
    tok, cot, slab, vecs, kid_col, seg_row, pad_row = (r[k] for k in NAMES_IN)
    out_ref, dtok_ref, g_out, v_out, vb_out = (r[k] for k in NAMES_OUT)
    X, N, DF, DA = r["X"], r["N"], r["DF"], r["DA"]
    Q, K, V, VT, KT, CTXT, CTX, DC = (r[k] for k in ("Q", "K", "V", "VT", "KT", "CTXT", "CTX", "DC"))
    PR, SC, ACTED, DP, XH, RST, FN = (r[k] for k in ("PR", "SC", "ACTED", "DP", "XH", "RST", "FN"))
    QST, DCST, CT, INNER = r["QST"], r["DCST"], r["CT"], r["INNER"]
    S1, R1, S2, R2 = r["S1"], r["R1"], r["S2"], r["R2"]
    VEC, VA, RVT, VB = r["VEC"], r["VA"], r["RVT"], r["VB"]
    ag_s, ag_r, rs_s, rs_r, vt_s, vt_r = (r[k] for k in ("ag_s", "ag_r", "rs_s", "rs_r", "vt_s", "vt_r"))
    lanes = {"qkv": (0, 3 * pad_w), "out": (3 * pad_w + 2 * F, pad_w), "up": (3 * pad_w, F), "down": (3 * pad_w + F, F)}

    f = lax.axis_index("fsdp")
    t = lax.axis_index("tensor")
    zs = n_f // 2
    z, y = f // 2, f % 2
    t1 = t + 1 - 2 * (t % 2)
    t2 = (t + 2) % 4
    t3 = t1 + 2 - 4 * (t1 // 2)
    yp = z * 2 + 1 - y

    def zpeer(k):
        return ((z + k) % zs) * 2 + y

    def rows(j):
        return pl.ds(pl.multiple_of(j * R, R), R)

    sent = []

    def send(src, dst, ss, rs, to):
        c = pltpu.make_async_remote_copy(
            src_ref=src, dst_ref=dst, send_sem=ss, recv_sem=rs, device_id=to, device_id_type=MESH
        )
        c.start()
        sent.append(c)
        return c

    def arrived(dst, ss, rs):
        pltpu.make_async_remote_copy(
            src_ref=dst, dst_ref=dst, send_sem=ss, recv_sem=rs, device_id=(f, t1), device_id_type=MESH
        ).wait_recv()

    barrier = pltpu.get_barrier_semaphore()
    peers = [(f, t1), (f, t2), (f, t3)]
    if fused:
        peers += [(yp, t)] + [(zpeer(k), t) for k in range(1, zs)]
    for p in peers:
        pl.semaphore_signal(barrier, inc=1, device_id=p, device_id_type=MESH)
    pl.semaphore_wait(barrier, len(peers))

    def gather_start(i, src, full):
        send(src, full.at[rows(t)], ag_s.at[i, 1], ag_r.at[i, 1], (f, t2))
        send(src, full.at[rows(t)], ag_s.at[i, 0], ag_r.at[i, 0], (f, t1))

    def gather_steps(i, full):
        yield t
        arrived(full.at[rows(t1)], ag_s.at[i, 0], ag_r.at[i, 0])
        yield t1
        arrived(full.at[rows(t2)], ag_s.at[i, 1], ag_r.at[i, 1])
        send(full.at[rows(t2)], full.at[rows(t2)], ag_s.at[i, 2], ag_r.at[i, 2], (f, t1))
        yield t2
        arrived(full.at[rows(t3)], ag_s.at[i, 2], ag_r.at[i, 2])
        yield t3

    def scatter_sum(i, part, between=None):
        S1[0] = part(t3).astype(narrow)
        a = send(S1.at[0], R1.at[0], rs_s.at[i, 0], rs_r.at[i, 0], (f, t1))
        far = part(t2)
        arrived(R1.at[0], rs_s.at[i, 0], rs_r.at[i, 0])
        S2[...] = (far + R1[0].astype(wide)).astype(narrow)
        b = send(S2, R2, rs_s.at[i, 2], rs_r.at[i, 2], (f, t2))
        S1[1] = part(t1).astype(narrow)
        c = send(S1.at[1], R1.at[1], rs_s.at[i, 1], rs_r.at[i, 1], (f, t1))
        dtok_ref[...] = part(t)
        if between is not None:
            between()
        arrived(R1.at[1], rs_s.at[i, 1], rs_r.at[i, 1])
        arrived(R2, rs_s.at[i, 2], rs_r.at[i, 2])
        done = (a, b, c)
        for d in done:
            d.wait_send()
        sent[:] = [c for c in sent if all(c is not d for d in done)]

    def summed(at):
        return dtok_ref[at, :] + R1[1, at, :].astype(wide) + R2[at, :].astype(wide)

    gather_start(0, tok, X)
    X[rows(t), :] = tok[...]
    if fused:
        W, VG, w_s, w_r = r["W"], r["VG"], r["w_s"], r["w_r"]

        def shard_rows(ff):
            return pl.ds(pl.multiple_of(ff * shard, shard), shard)

        def w_at(p, ff):
            lo, n = lanes[p]
            return W.at[shard_rows(ff), pl.ds(lo, n)]

        def w_own(p, i):
            lo, n = lanes[p]
            src = slab.at[:, pl.ds(lo, n)]
            for k in range(1, zs):
                send(src, w_at(p, f), w_s.at[i, k - 1], w_r.at[i, k - 1], (zpeer(k), t))
            send(src, w_at(p, f), w_s.at[i, zs - 1], w_r.at[i, zs - 1], (yp, t))

        def w_forward(p, i):
            for k in range(1, zs):
                ff = zpeer(zs - k)
                arrived(w_at(p, ff), w_s.at[i, k - 1], w_r.at[i, k - 1])
                send(w_at(p, ff), w_at(p, ff), w_s.at[i, zs - 1 + k], w_r.at[i, zs - 1 + k], (yp, t))

        def w_finish(p, i):
            arrived(w_at(p, yp), w_s.at[i, zs - 1], w_r.at[i, zs - 1])
            for k in range(1, zs):
                ff = ((z + zs - k) % zs) * 2 + 1 - y
                arrived(w_at(p, ff), w_s.at[i, zs - 1 + k], w_r.at[i, zs - 1 + k])

        n_p = len(PARTS)
        w_own("qkv", 0)
        for k in range(1, zs):
            send(vecs, VG.at[f], w_s.at[n_p, k - 1], w_r.at[n_p, k - 1], (zpeer(k), t))
        send(vecs, VG.at[f], w_s.at[n_p, zs - 1], w_r.at[n_p, zs - 1], (yp, t))
        for i in range(1, n_p):
            w_own(PARTS[i], i)
        W[shard_rows(f), :] = slab[...]
        VG[f] = vecs[...]
        w_forward("qkv", 0)
        for k in range(1, zs):
            ff = zpeer(zs - k)
            arrived(VG.at[ff], w_s.at[n_p, k - 1], w_r.at[n_p, k - 1])
            send(VG.at[ff], VG.at[ff], w_s.at[n_p, zs - 1 + k], w_r.at[n_p, zs - 1 + k], (yp, t))
        w_finish("qkv", 0)
        arrived(VG.at[yp], w_s.at[n_p, zs - 1], w_r.at[n_p, zs - 1])
        for k in range(1, zs):
            ff = ((z + zs - k) % zs) * 2 + 1 - y
            arrived(VG.at[ff], w_s.at[n_p, zs - 1 + k], w_r.at[n_p, zs - 1 + k])
        total = VG[0].astype(wide)
        for k in range(1, n_f):
            total = total + VG[k].astype(wide)
        VEC[...] = total
    else:
        W = slab
        VEC[...] = vecs[...].astype(wide)

    def weight(p):
        lo, n = lanes[p]
        return W[:, lo : lo + n]

    wq = pad_w
    for j in gather_steps(0, X):
        got = nn(X[rows(j), :], weight("qkv"))
        Q[rows(j), :] = (got[:, :wq] + VEC[7:8, :wq]).astype(narrow) * narrow(0.125)
        keys = got[:, wq : 2 * wq]
        values = got[:, 2 * wq : 3 * wq] + VEC[8:9, :wq]
        K[rows(j), :] = keys.astype(narrow)
        V[rows(j), :] = values.astype(narrow)
        KT[:, rows(j)] = keys.T.astype(narrow)
        VT[:, rows(j)] = values.T.astype(narrow)

    nb = S // BLK
    reach = (DOC_MOST + BLK - 2) // BLK
    spans = [(max(0, b - reach), min(nb, b + reach + 1)) for b in range(nb)]
    offs = [sum(hi - lo for lo, hi in spans[:b]) for b in range(nb)]

    def stack_heads(dst, value):
        lane = lax.broadcasted_iota(jnp.int32, value.shape, 1) // DH
        for h in range(heads):
            dst[h * BLK : (h + 1) * BLK, :] = jnp.where(lane == h, value, 0).astype(narrow)

    def krows(kc):
        return pl.ds(pl.multiple_of(kc * BLK, BLK), BLK)

    def attend(b):
        lo, hi = spans[b]
        q0 = b * BLK
        stack_heads(QST, Q[q0 : q0 + BLK, :].astype(wide))
        seg_q = seg_row[:, q0 : q0 + BLK]
        pos_q = q0 + lax.broadcasted_iota(jnp.int32, (1, BLK), 1)

        def scores(kc, top):
            s = nt(K[krows(kc), :], QST[...])
            kid = kid_col[krows(kc), :]
            pos_k = kc * BLK + lax.broadcasted_iota(jnp.int32, (BLK, 1), 0)
            allowed = (kid == seg_q) | (pos_k == pos_q)
            bias = jnp.where(allowed, 0.0, MASKED)
            s = s + jnp.concatenate([bias] * heads, axis=1)
            SC[krows(kc), :] = s
            return jnp.maximum(top, jnp.max(s, axis=0, keepdims=True))

        top = lax.fori_loop(lo, hi, scores, jnp.full((1, heads * BLK), -3e38, wide))

        def exps(kc, total):
            e = jnp.exp(SC[krows(kc), :] - top)
            SC[krows(kc), :] = e
            return total + jnp.sum(e, axis=0, keepdims=True)

        total = lax.fori_loop(lo, hi, exps, jnp.zeros((1, heads * BLK), wide))
        inv = 1.0 / total
        CT[...] = jnp.zeros_like(CT)

        def contexts(kc, carry):
            p = (SC[krows(kc), :] * inv).astype(narrow)
            PR[offs[b] + kc - lo] = p
            for h in range(heads):
                hd = slice(h * DH, (h + 1) * DH)
                CT[hd, :] += nn(VT[hd, krows(kc)], p[:, h * BLK : (h + 1) * BLK])
            return carry

        lax.fori_loop(lo, hi, contexts, 0)
        ct = CT[...] * pad_row[:, q0 : q0 + BLK].astype(wide)
        CTXT[:, q0 : q0 + BLK] = ct
        CTX[q0 : q0 + BLK, :] = ct.T.astype(narrow)

    for b in range(nb):
        attend(b)
        if fused and b == nb // 2:
            w_forward("out", 1)
        if fused and b == nb - 1:
            w_forward("up", 2)
            w_finish("out", 1)

    def mine(at, n=LN_ROWS):
        return kid_col[pl.ds(pl.multiple_of(t * R + at, n), n), :] >= 0

    VA[...] = jnp.zeros_like(VA)
    scatter_sum(0, lambda j: nt(CTX[rows(j), :], weight("out")), (lambda: w_forward("down", 3)) if fused else None)

    def add(row, value):
        VA[row : row + 1, :] += jnp.sum(value, axis=0, keepdims=True)

    def mean(v):
        return jnp.mean(v, axis=-1, keepdims=True)

    def norm(h):
        centered = h - mean(h)
        rstd = lax.rsqrt(mean(centered * centered) + EPSILON)
        return centered * rstd, rstd

    def chunked(body):
        def step(i, carry):
            at = pl.multiple_of(i * LN_ROWS, LN_ROWS)
            body(pl.ds(at, LN_ROWS), pl.ds(pl.multiple_of(t * R + at, LN_ROWS), LN_ROWS), at)
            return carry

        lax.fori_loop(0, R // LN_ROWS, step, 0)

    def first(at, whole_at, start):
        branch = summed(at) + VEC[5:6, :]
        x = tok[at, :].astype(wide)
        xh, rstd = norm(x + branch)
        XH[at, :] = xh
        RST[at, :] = rstd
        fn = xh * VEC[1:2, :] + VEC[3:4, :]
        FN[at, :] = fn
        N[whole_at, :] = fn.astype(narrow)
        live = jnp.where(mine(start), 1.0, 0.0)
        add(7, live * x * x)
        add(8, live * branch * branch)
        add(10, jnp.broadcast_to(live, x.shape))

    chunked(first)
    gather_start(1, N.at[rows(t)], N)
    if fused:
        w_finish("up", 2)

    def up_block(j):
        pre = nn(N[rows(j), :], weight("up")) + VEC[0:1, :F]
        half = 0.5 * (1.0 + lax.erf(pre * 0.7071067811865476))
        ACTED[rows(j), :] = (pre * half).astype(narrow)
        SC[rows(j), :] = half + pre * jnp.exp(-0.5 * pre * pre) * 0.3989422804014327

    for j in gather_steps(1, N):
        up_block(j)
    if fused:
        w_finish("down", 3)
    scatter_sum(1, lambda j: nt(ACTED[rows(j), :], weight("down")))

    def back_norm(dy, xh, rstd, gain):
        d = dy * gain
        return rstd * (d - mean(d) - xh * mean(d * xh))

    def second(at, whole_at, start):
        branch = summed(at) + VEC[6:7, :]
        xh, rstd = norm(FN[at, :] + branch)
        gain = VEC[2:3, :]
        out_ref[at, :] = (xh * gain + VEC[4:5, :]).astype(narrow)
        live = jnp.where(mine(start), 1.0, 0.0)
        add(9, live * branch * branch)
        dy = cot[at, :].astype(wide)
        add(2, dy * xh)
        add(4, dy)
        d_second = back_norm(dy, xh, rstd, gain)
        FN[at, :] = d_second
        low = d_second.astype(narrow)
        DF[whole_at, :] = low
        add(6, low.astype(wide))

    chunked(second)
    gather_start(2, DF.at[rows(t)], DF)

    def d_pre_block(j):
        d = (nn(DF[rows(j), :], weight("down")) * SC[rows(j), :]).astype(narrow)
        DP[rows(j), :] = d
        VA[0:1, :F] += jnp.sum(d.astype(wide), axis=0, keepdims=True)

    for j in gather_steps(2, DF):
        d_pre_block(j)

    G = r["G"] if fused else g_out

    def grad(p, left, right):
        lo, n = lanes[p]
        step_w = 256

        def step(i, carry):
            at = pl.ds(pl.multiple_of(i * step_w, step_w), step_w)
            G[at, lo : lo + n] = tn(left[:, at], right[...]).astype(narrow)
            return carry

        lax.fori_loop(0, D // step_w, step, 0)
        if fused:
            i = PARTS.index(p)
            for zz in range(zs):
                send(
                    G.at[shard_rows(zz * 2 + 1 - y), pl.ds(lo, n)],
                    RY.at[zz, :, pl.ds(lo, n)],
                    g_s.at[i, zz],
                    g_r.at[i, zz],
                    (yp, t),
                )

    def grad_across(p):
        if not fused:
            return
        lo, n = lanes[p]
        i = PARTS.index(p)
        for zz in range(zs):
            arrived(RY.at[zz, :, pl.ds(lo, n)], g_s.at[i, zz], g_r.at[i, zz])
            both = G[shard_rows(zz * 2 + y), lo : lo + n].astype(wide) + RY[zz, :, lo : lo + n].astype(wide)
            RY[zz, :, lo : lo + n] = both.astype(narrow)
        for k in range(1, zs):
            send(
                RY.at[(z + k) % zs, :, pl.ds(lo, n)],
                RZ.at[k - 1, :, pl.ds(lo, n)],
                g_s.at[i, zs + k - 1],
                g_r.at[i, zs + k - 1],
                (zpeer(k), t),
            )

    def grad_finish(p):
        if not fused:
            return
        lo, n = lanes[p]
        i = PARTS.index(p)
        got = RY[z, :, lo : lo + n].astype(wide)
        for k in range(1, zs):
            arrived(RZ.at[k - 1, :, pl.ds(lo, n)], g_s.at[i, zs + k - 1], g_r.at[i, zs + k - 1])
            got = got + RZ[k - 1, :, lo : lo + n].astype(wide)
        g_out[:, lo : lo + n] = got

    if fused:
        RY, RZ, g_s, g_r = (r[k] for k in ("RY", "RZ", "g_s", "g_r"))

    scatter_sum(2, lambda j: nt(DP[rows(j), :], weight("up")), lambda: grad("down", DF, ACTED))

    def first_back(at, whole_at, start):
        dy = FN[at, :] + summed(at)
        xh = XH[at, :]
        add(1, dy * xh)
        add(3, dy)
        d_first = back_norm(dy, xh, RST[at, :], VEC[1:2, :])
        FN[at, :] = d_first
        low = d_first.astype(narrow)
        DA[whole_at, :] = low
        add(5, low.astype(wide))

    chunked(first_back)
    gather_start(3, DA.at[rows(t)], DA)
    for k, tt in enumerate((t1, t2, t3)):
        send(VA, RVT.at[t], vt_s.at[k], vt_r.at[k], (f, tt))
    grad("up", N, DP)

    def d_context_block(j):
        live = jnp.where(kid_col[rows(j), :] >= 0, 1.0, 0.0)
        DC[rows(j), :] = (nn(DA[rows(j), :], weight("out")) * live).astype(narrow)

    for j in gather_steps(3, DA):
        d_context_block(j)
    grad_across("down")

    RVT[t] = VA[...]
    for k, tt in enumerate((t1, t2, t3)):
        arrived(RVT.at[tt], vt_s.at[k], vt_r.at[k])
    both = RVT[0] + RVT[1] + RVT[2] + RVT[3]
    row = lax.broadcasted_iota(jnp.int32, both.shape, 0)
    both = jnp.where(row == 0, VA[...], both)
    if fused:
        RVY, RVZ, vf_s, vf_r = (r[k] for k in ("RVY", "RVZ", "vf_s", "vf_r"))
        RVY[y] = both
        send(RVY.at[y], RVY.at[y], vf_s.at[0], vf_r.at[0], (yp, t))
    else:
        v_out[...] = both

    SC[...] = jnp.zeros_like(SC)
    dk_at, dv_at = slice(0, wq), slice(wq, 2 * wq)

    def attend_back(b):
        lo, hi = spans[b]
        q0 = b * BLK
        stack_heads(QST, Q[q0 : q0 + BLK, :].astype(wide))
        dc = DC[q0 : q0 + BLK, :].astype(wide)
        stack_heads(DCST, dc)
        prod = dc.T * CTXT[:, q0 : q0 + BLK]
        for h in range(heads):
            INNER[:, h * BLK : (h + 1) * BLK] = jnp.sum(prod[h * DH : (h + 1) * DH, :], axis=0, keepdims=True)
        CT[...] = jnp.zeros_like(CT)

        def step(kc, carry):
            p = PR[offs[b] + kc - lo]
            dp = nt(V[krows(kc), :], DCST[...])
            ds = (p.astype(wide) * (dp - INNER[...])).astype(narrow)
            SC[krows(kc), dv_at] += nn(p, DCST[...])
            SC[krows(kc), dk_at] += nn(ds, QST[...])
            for h in range(heads):
                hd = slice(h * DH, (h + 1) * DH)
                CT[hd, :] += nn(KT[hd, krows(kc)], ds[:, h * BLK : (h + 1) * BLK])
            return carry

        lax.fori_loop(lo, hi, step, 0)
        DP[q0 : q0 + BLK, :wq] = (CT[...].T * 0.125).astype(narrow)

    for b in range(nb):
        attend_back(b)
        if b == 0 and fused:
            grad_across("up")
            arrived(RVY.at[1 - y], vf_s.at[0], vf_r.at[0])
            RVZ[z] = RVY[0] + RVY[1]
            for k in range(1, zs):
                send(RVZ.at[z], RVZ.at[z], vf_s.at[k], vf_r.at[k], (zpeer(k), t))
        if b == 1:
            grad("out", DA, CTX)
        if b == 3:
            grad_across("out")
    DP[:, wq : 2 * wq] = SC[:, dk_at].astype(narrow)
    DP[:, 2 * wq : 3 * wq] = SC[:, dv_at].astype(narrow)
    VB[0:1, :] = jnp.sum(DP[:, :wq].astype(wide), axis=0, keepdims=True)
    VB[1:2, :] = jnp.sum(DP[:, 2 * wq : 3 * wq].astype(wide), axis=0, keepdims=True)
    if fused:
        VBG, vb_s, vb_r = r["VBG"], r["vb_s"], r["vb_r"]
        VBG[f] = VB[...]
        ks = list(range(1, n_f))
        for k in ks:
            send(VB, VBG.at[f], vb_s.at[k - 1], vb_r.at[k - 1], ((f + k) % n_f, t))
    else:
        vb_out[...] = VB[...]

    def finish():
        grad("qkv", X, DP.at[:, pl.ds(0, 3 * wq)])
        grad_across("qkv")
        for p in ("down", "up", "out"):
            grad_finish(p)

    scatter_sum(3, lambda j: nt(DP[rows(j), : 3 * wq], weight("qkv")), finish)

    def last(at, whole_at, start):
        dtok_ref[at, :] = FN[at, :] + summed(at)

    chunked(last)
    if fused:
        for k in range(1, zs):
            zz = (z + zs - k) % zs
            arrived(RVZ.at[zz], vf_s.at[k], vf_r.at[k])
        v_out[...] = sum((RVZ[k] for k in range(1, zs)), RVZ[0])
        for k in range(1, n_f):
            arrived(VBG.at[(f + n_f - k) % n_f], vb_s.at[k - 1], vb_r.at[k - 1])
        vb_out[...] = sum((VBG[k] for k in range(1, n_f)), VBG[0])
        grad_finish("qkv")
    for c in sent:
        c.wait_send()


NAMES_IN = ("tok", "cot", "slab", "vecs", "kid_col", "seg_row", "pad_row")
NAMES_OUT = ("out_ref", "dtok_ref", "g_out", "v_out", "vb_out")
NAMES_SCRATCH = []


def scratch_of(fused, n_f, D, F, S, heads, pad_w, shard):
    R = S // 4
    nb = S // BLK
    reach = (DOC_MOST + BLK - 2) // BLK
    tiles = sum(min(nb, b + reach + 1) - max(0, b - reach) for b in range(nb))
    width = 3 * pad_w + 2 * F + pad_w
    zs = n_f // 2
    vm, dma = pltpu.VMEM, pltpu.SemaphoreType.DMA
    out = dict(
        X=vm((S, D), narrow),
        N=vm((S, D), narrow),
        DF=vm((S, D), narrow),
        DA=vm((S, D), narrow),
        Q=vm((S, pad_w), narrow),
        K=vm((S, pad_w), narrow),
        V=vm((S, pad_w), narrow),
        VT=vm((pad_w, S), narrow),
        KT=vm((pad_w, S), narrow),
        CTXT=vm((pad_w, S), wide),
        CTX=vm((S, pad_w), narrow),
        DC=vm((S, pad_w), narrow),
        PR=vm((tiles, BLK, heads * BLK), narrow),
        SC=vm((S, max(heads * BLK, F)), wide),
        ACTED=vm((S, F), narrow),
        DP=vm((S, max(F, 3 * pad_w)), narrow),
        XH=vm((R, D), wide),
        RST=vm((R, 1), wide),
        FN=vm((R, D), wide),
        QST=vm((heads * BLK, pad_w), narrow),
        DCST=vm((heads * BLK, pad_w), narrow),
        CT=vm((pad_w, BLK), wide),
        INNER=vm((1, heads * BLK), wide),
        S1=vm((2, R, D), narrow),
        R1=vm((2, R, D), narrow),
        S2=vm((R, D), narrow),
        R2=vm((R, D), narrow),
        VEC=vm((16, D), wide),
        VA=vm((16, D), wide),
        RVT=vm((4, 16, D), wide),
        VB=vm((8, pad_w), wide),
        ag_s=dma((4, 3)),
        ag_r=dma((4, 3)),
        rs_s=dma((4, 3)),
        rs_r=dma((4, 3)),
        vt_s=dma((3,)),
        vt_r=dma((3,)),
    )
    if fused:
        out.update(
            W=vm((D, width), narrow),
            VG=vm((n_f, 16, D), narrow),
            G=vm((D, width), narrow),
            RY=vm((zs, shard, width), narrow),
            RZ=vm((zs - 1, shard, width), narrow),
            RVY=vm((2, 16, D), wide),
            RVZ=vm((zs, 16, D), wide),
            VBG=vm((n_f, 8, pad_w), wide),
            w_s=dma((5, 2 * zs - 1)),
            w_r=dma((5, 2 * zs - 1)),
            g_s=dma((4, 2 * zs - 1)),
            g_r=dma((4, 2 * zs - 1)),
            vf_s=dma((zs,)),
            vf_r=dma((zs,)),
            vb_s=dma((n_f - 1,)),
            vb_r=dma((n_f - 1,)),
        )
    return out


def shards(
    tokens,
    attn_weight,
    query_value_bias,
    out_weight,
    hidden_weight,
    hidden_bias,
    down_weight,
    norm_gains,
    norm_biases,
    output_biases,
    segment_ids,
    padding,
    cotangent,
):
    n_f = lax.axis_size("fsdp")
    f = lax.axis_index("fsdp")
    R, D = tokens.shape
    S = segment_ids.shape[0]
    F = hidden_weight.shape[1]
    shard = hidden_weight.shape[0]
    heads = query_value_bias.shape[1]
    hw = heads * DH
    pad_w = -(-hw // 128) * 128
    fused = n_f == 8 and shard % 16 == 0
    sizes = (fused, n_f, D, F, S, heads, pad_w, shard)

    def padded(a):
        return jnp.pad(a, ((0, 0), (0, pad_w - hw)))

    slab = jnp.concatenate(
        [padded(attn_weight[0]), padded(attn_weight[1]), padded(attn_weight[2])]
        + [hidden_weight, down_weight.T, padded(out_weight.T)],
        axis=1,
    )
    here = (jnp.arange(n_f) == f).astype(narrow)

    def spread(a):
        return (a[:, None, :] * here[None, :, None]).reshape(a.shape[0], -1)

    def row_of(a):
        flat = a.reshape(1, -1)
        return jnp.pad(flat, ((0, 0), (0, D - flat.shape[1])))

    vecs = jnp.concatenate(
        [row_of(spread(hidden_bias))]
        + [spread(norm_gains), spread(norm_biases), spread(output_biases)]
        + [row_of(spread(query_value_bias[0])), row_of(spread(query_value_bias[1]))]
        + [jnp.zeros((7, D), narrow)],
        axis=0,
    )
    if not fused:
        slab = lax.all_gather(slab, "fsdp", axis=0, tiled=True)
        vecs = lax.psum(vecs.astype(wide), "fsdp").astype(narrow)
    kid_col = jnp.where(padding == 1, segment_ids, -1)[:, None]
    width = slab.shape[1]
    scratch = scratch_of(*sizes)
    NAMES_SCRATCH[:] = list(scratch)
    vm = pl.BlockSpec(memory_space=pltpu.VMEM)
    g_shape = jax.ShapeDtypeStruct((shard, width), wide) if fused else jax.ShapeDtypeStruct((D, width), narrow)
    layer_out, d_tokens, g, v, vb = pl.pallas_call(
        functools.partial(layer_kernel, sizes),
        out_shape=(
            jax.ShapeDtypeStruct((R, D), narrow),
            jax.ShapeDtypeStruct((R, D), wide),
            g_shape,
            jax.ShapeDtypeStruct((16, D), wide),
            jax.ShapeDtypeStruct((8, pad_w), wide),
        ),
        in_specs=[vm] * 7,
        out_specs=[vm] * 5,
        scratch_shapes=list(scratch.values()),
        compiler_params=pltpu.CompilerParams(
            collective_id=0, has_side_effects=True, vmem_limit_bytes=67043328
        ),
    )(tokens, cotangent, slab, vecs, kid_col, segment_ids[None, :], padding[None, :])
    if not fused:
        blocks = g.reshape(n_f, shard, width)
        g = lax.all_to_all(blocks, "fsdp", split_axis=0, concat_axis=0, tiled=True).astype(wide).sum(axis=0)
        v = lax.psum(v, "fsdp")
        vb = lax.psum(vb, "fsdp")

    def mine(a, k):
        return lax.dynamic_slice_in_dim(a.reshape(k, n_f, -1), f, 1, 1)[:, 0]

    d_attn = jnp.stack([g[:, k * pad_w : k * pad_w + hw] for k in range(3)])
    base = 3 * pad_w
    d_bias = mine(vb[:2, :hw].reshape(2 * heads, DH), 2 * heads).reshape(2, heads, -1)
    squares = jnp.sum(v[7:10], axis=1)
    return (
        layer_out,
        d_tokens,
        d_attn,
        d_bias,
        g[:, base + 2 * F : base + 2 * F + hw].T,
        g[:, base : base + F],
        mine(v[0, :F].reshape(-1, DH), F // DH),
        g[:, base + F : base + 2 * F].T,
        mine(v[1:3], 2),
        mine(v[3:5], 2),
        mine(v[5:7], 2),
        jnp.sqrt(squares / (v[10, 0] * D)),
    )


def solution(mesh):
    placed = (
        P(("fsdp", "tensor"), None),
        P(None, "fsdp", "tensor"),
        P(None, "tensor", "fsdp"),
        P("tensor", "fsdp"),
        P("fsdp", "tensor"),
        P("tensor", "fsdp"),
        P("tensor", "fsdp"),
        P(None, "fsdp"),
        P(None, "fsdp"),
        P(None, "fsdp"),
        P("fsdp"),
        P("fsdp"),
        P(("fsdp", "tensor"), None),
    )
    return jax.shard_map(
        shards,
        mesh=mesh,
        in_specs=placed,
        out_specs=(
            P(("fsdp", "tensor"), None),
            P(("fsdp", "tensor"), None),
            P(None, "fsdp", "tensor"),
            P(None, "tensor", "fsdp"),
            P("tensor", "fsdp"),
            P("fsdp", "tensor"),
            P("tensor", "fsdp"),
            P("tensor", "fsdp"),
            P(None, "fsdp"),
            P(None, "fsdp"),
            P(None, "fsdp"),
            P(),
        ),
        check_vma=False,
    )
```

time: 722 us -> 254 us (0.35)
  blocking collectives: 238 us -> 0 us
  Pallas kernels: 0 us -> 218 us
  waiting for transfers between devices: 163 us -> 0 us
  matrix products: 135 us -> 0 us
  other arithmetic: 80.1 us -> 3.07 us
  starting transfers between devices: 29.7 us -> 0 us
  between operations: 17 us -> 1.46 us
  local copies, waits for them, and re-layouts: 39.1 us -> 27.3 us
  loops' own time: 10.2 us -> 0 us
    pallas_call x0 -> x1, Pallas kernels: none -> 218 us  [shards(): pl.pallas_call(functools.partial(layer_kernel, sizes), out_shape=(jax.Sha...]
    all_gather x7 -> x0, blocking collectives: 181 us -> none  [the longest x1 38.2 us: shards(): lax.all_gather(attn_weight, 'fsdp', axis=1, tiled=True)]
    dot_general x33 -> x0, matrix products: 135 us -> none  [the longest x6 27.7 us: scores_of(): jnp.einsum('qhd,khd->hqk', q_rows, all_keys, preferred_element_type=wide)]
    reduce_scatter x4 -> x0, waiting for transfers between devices: 78.5 us -> none  [the longest x1 48.1 us: shards(): lax.psum_scatter(d_norm_part, 'tensor', scatter_dimension=0, tiled=True)]
    psum x2 -> x0, blocking collectives: 57.2 us -> none  [the longest x1 45.6 us: shards(): lax.psum((squares, jnp.sum(local_pad)), ('fsdp', 'tensor'))]
    all_gather x6 -> x0, waiting for transfers between devices: 46.1 us -> none  [the longest x1 23.8 us: shards(): d_ff_all = lax.all_gather(d_ff_low, 'tensor', axis=0, tiled=True)]
    all_to_all x6 -> x0, waiting for transfers between devices: 36.7 us -> none  [summed_on_arrival(): lax.all_to_all(blocks, axis, split_axis=0, concat_axis=0, tiled=True)]
    convert_element_type x12 -> x1, other arithmetic: 32.3 us -> 0.01 us  [shards(): here = (jnp.arange(n_f) == f).astype(narrow)]
  transfers between devices with their start and end apart: 16 -> 0, of which waited for: 7 -> 0; matrix products, arithmetic and copies ran while one was open for 24% -> 0% of each run, Pallas kernels for 0% -> 0%
where the time goes in v1:
time: 254 us; the launch traced here: 250 us
  Pallas kernels  218 us (86%)
  local copies, waits for them, and re-layouts  27.3 us (11%)
  other arithmetic  3.07 us (1%)
    pallas_call x1, Pallas kernels, shards(): pl.pallas_call(functools.partial(layer_kernel, sizes), out_shape=(jax.Sha...  218 us
    unnamed x20, local copies, waits for them, and re-layouts  8.96 us

profile of v1, /device:TPU:0, one launch (start us, length us, event | category | flops | bytes accessed | tf_op | source)
XLA Modules:
  0.0 249.9 jit_solution(13801269456480044665)
XLA Ops:
  0.7 0.1 mul.132
  0.8 0.8 fusion.1
  1.6 0.8 copy.32
  2.4 0.7 mul.129
  3.0 0.1 mul.130
  3.1 0.7 mul.135
  3.8 0.1 mul.136
  3.9 0.7 mul.138
  4.5 0.1 mul.139
  4.6 1.3 broadcast_in_dim.15.refs_5_
  5.9 1.3 broadcast_in_dim.30.refs_6_
  7.2 0.7 compare_select_fusion
  8.0 0.1 mul.149
  8.1 0.1 mul.145
  8.3 0.1 mul.128
  8.4 1.3 concatenate.7.refs_3_
  9.7 0.9 copy.31
  10.6 0.9 slice_bitcast_fusion.5
  11.5 0.6 pad_dynamic-update-slice_fusion.3
  12.1 0.6 pad_dynamic-update-slice_fusion.2
  12.7 0.6 pad_dynamic-update-slice_fusion.1
  13.3 1.6 constant_dynamic-update-slice_fusion
  14.9 0.7 bitcast_dynamic-update-slice_fusion
  15.6 0.6 pad_dynamic-update-slice_fusion.refs_2_
  16.2 1.1 broadcast_in_dim.31.refs_4_
  17.4 218.1 %shard_map.220 = (bf16[384,768]{1,0:T(8,128)(2,1)}, f32[384,768]{1,0:T(8,128)}, f32[96,2560]{1,0:T(8,128)}, f32[16,768]{1,0:T(8,128)}, f32[8,256]{1,0:T(8,128)}) custom-call(bf16[384,768]{1,0:T(8,128)(2,1)} %refs_0_.1, bf16[384,768]{1,0:T(8,128)(2,1)} %refs_1_.1, bf16[96,2560]{1,0:T(8,128)(2,1)} %pad_dynamic-update-slice_fusion.refs_2_, ...), custom_call_target="tpu_custom_call" | custom-call | tf_op jit(solution)/shard_map/pallas_call | solution.py:654
  235.5 1.3 slice.71
  237.4 0.9 slice_reduce_fusion
  238.3 0.5 divide_sqrt_fusion
  238.9 0.7 slice.62
  239.6 0.8 slice_reduce_fusion.1
  240.3 0.9 fusion
  241.2 0.1 reshape.123
  241.2 0.6 constant_dynamic-slice_fusion
  241.8 0.1 reshape.122
  241.9 0.6 constant_dynamic-slice_fusion.1
  242.5 0.1 reshape.121
  242.6 0.6 constant_dynamic-slice_fusion.2
  243.1 0.1 reshape_reshape.2
  243.3 0.6 copy.36
  243.8 0.1 reshape_reshape_squeeze.3
  243.9 0.7 copy.35
  244.6 1.1 slice_bitcast_fusion.1
  245.7 0.9 slice_bitcast_fusion
  246.6 0.7 copy.37
  247.3 0.7 pad_maximum_fusion
  248.0 0.8 copy.51
  248.8 1.0 copy.52
  (20 shorter events, 0.3 us)
Async XLA Ops:
  0.6 14.3 %copy-start.3 = (bf16[768,96]{0,1:T(8,128)(2,1)S(1)}, bf16[768,96]{0,1:T(8,128)(2,1)}, u32[]{:S(2)}) copy-start(bf16[768,96]{0,1:T(8,128)(2,1)} %param.19) | copy-start | bytes 442372
  235.5 10.2 %copy-start.1 = (f32[96,2560]{1,0:T(8,128)S(1)}, f32[96,2560]{1,0:T(8,128)}, u32[]{:S(2)}) copy-start(f32[96,2560]{1,0:T(8,128)} %get-tuple-element.19) | copy-start | bytes 2949124
  245.7 2.3 copy-start.2
  246.5 2.3 copy-start
